TPU v7x, 128 devices: a whole 4x4x4 slice. The times are simulated.
128 devices in a mesh: group: 4 (over x_lo, core), bl: 32 (over x_hi, y, z).
Axes of the slice: x: 4 (x_hi: 2, x_lo: 2; x = x_hi * 2 + x_lo), y: 4, z: 4, core: 2. Of those that a mesh axis runs over, the one named last changes fastest.
Arguments:
- visibilities: float32 [2, 2048, 16, 1024], P(None, ('group', 'bl')), parts along dimension 1, may hold values from -400 to 400
- flags: int32 [2048, 8], P(('group', 'bl')), parts along dimension 0, may hold values 0 or 1
Outputs:
- cross_power: float32 [32, 2048, 512], P(None, ('group', 'bl')), parts along dimension 1
- bandpower: float32 [128], P('group'), parts along dimension 0
There are 4 independent parts, one for each index of `group`. A program takes and returns all parts, laid end to end along the dimension named above; each array names one. Nothing has to cross between parts.
All inputs are finite; a program needn't handle non-finite values. No bound on the sum of `flags` on one device may be relied on, other than what follows from the above.
Results may differ from a plain program's by a relative error of at most 0.004.
Values may be sent and summed in bfloat16 or wider, within the bound.
No kernel may reach another device: no remote copies, remote signals or barrier semaphores. Data moves between devices by JAX's collectives and lax.ppermute only.
A program may use at most 192 MiB of HBM per device.

v0:
```python
import math

import jax
import jax.numpy as jnp
from jax import lax
from jax.sharding import PartitionSpec as P

NF = 1024
NT = 16
CB = 128
BW = 32


def copy_for_each(array, axis):
    copies = jnp.broadcast_to(array, (lax.axis_size(axis), *array.shape))
    return lax.all_to_all(copies, axis, split_axis=0, concat_axis=0, tiled=True)


def taken_together(array, axis):
    return copy_for_each(array, axis).sum(axis=0)


def make_taper():
    angle = jnp.arange(NF, dtype=jnp.int32).astype(jnp.float32) * (2.0 * math.pi / (NF - 1))
    return (
        0.35875
        - 0.48829 * jnp.cos(angle)
        + 0.14128 * jnp.cos(2.0 * angle)
        - 0.01168 * jnp.cos(3.0 * angle)
    )


def make_tables():
    index = jnp.arange(NF, dtype=jnp.int32)
    phase = index[:, None] * index[None, :] % NF
    angle = phase.astype(jnp.float32) * (2.0 * math.pi / NF)
    return (jnp.cos(angle), jnp.sin(angle))


def delay_spectra(visibilities, flags):
    count = visibilities.shape[1]
    keep = (
        jnp.broadcast_to(flags[:, :, None], (count, NF // CB, CB))
        .reshape(count, NF)
        .astype(jnp.float32)
    )
    weight = keep * make_taper()[None, :]
    tapered = visibilities * weight[None, :, None, :]
    real_rows = tapered[0].reshape(count * NT, NF)
    imag_rows = tapered[1].reshape(count * NT, NF)
    cosine, sine = make_tables()
    high = lax.Precision.HIGHEST
    scale = 1.0 / math.sqrt(NF)
    real_out = (
        jnp.dot(real_rows, cosine, precision=high) + jnp.dot(imag_rows, sine, precision=high)
    ) * scale
    imag_out = (
        jnp.dot(imag_rows, cosine, precision=high) - jnp.dot(real_rows, sine, precision=high)
    ) * scale
    stacked = jnp.stack([real_out.reshape(count, NT, NF), imag_out.reshape(count, NT, NF)], 2)
    stacked = stacked.reshape(count, NT, 2, NF // BW, BW).transpose(3, 0, 1, 2, 4)
    return stacked.reshape(NF // BW, count, NT * 2 * BW).astype(jnp.bfloat16)


def shards(visibilities, flags):
    own = delay_spectra(visibilities, flags)
    bands, rows, inner = own.shape
    total = rows * lax.axis_size("bl")
    term = (
        jnp.einsum(
            "kbj,kcj->kbc",
            own,
            lax.all_gather(own, "bl", axis=1, tiled=True),
            preferred_element_type=jnp.float32,
        )
        / NT
    )
    own_wide = own.astype(jnp.float32)
    self_power = jnp.sum(own_wide * own_wide, axis=2) / NT
    partial_sum = jnp.sum(term, axis=(1, 2)) - jnp.sum(self_power, axis=1)
    bandpower = taken_together(partial_sum, "bl") / total
    return (term, bandpower)


def solution(mesh):
    return jax.shard_map(
        shards,
        mesh=mesh,
        in_specs=(P(None, ("group", "bl"), None, None), P(("group", "bl"), None)),
        out_specs=(P(None, ("group", "bl"), None), P("group")),
        check_vma=False,
    )
```

profile of v0, /device:TPU:0, one launch (start us, length us, event | category | flops | bytes accessed | tf_op | source)
XLA Modules:
  0.0 420.4 jit_solution(16420377505746367192)
XLA Ops:
  7.2 0.0 all-gather.2.cloned.1.call-start
  7.2 0.1 multiply_subtract_fusion
  7.3 0.7 convert_element_type.43
  8.0 0.1 copy.8
  8.0 0.1 broadcast_in_dim.4
  8.1 1.8 broadcast_multiply_fusion
  10.0 0.2 fusion.45
  10.2 20.0 %fusion.8 = f32[256,1024]{1,0:T(8,128)S(1)} fusion(f32[256,1024]{1,0:T(8,128)S(1)} %bitcast.14), kind=kOutput, calls=%fused_computation.13 | convolution fusion | flops 3235905536 | bytes 2097152 | tf_op jit(solution)/shard_map/dot_general | solution.py:58
  30.2 20.0 %fusion.10 = f32[256,1024]{1,0:T(8,128)S(1)} fusion(f32[256,1024]{1,0:T(8,128)S(1)} %bitcast.16), kind=kOutput, calls=%fused_computation.14 | convolution fusion | flops 3235905536 | bytes 2097152 | tf_op jit(solution)/shard_map/dot_general | solution.py:55
  50.2 19.7 %fusion.22 = bf16[256,1024]{1,0:T(8,128)(2,1)S(1)} fusion(f32[256,1024]{1,0:T(8,128)S(1)} %fusion.8, f32[256,1024]{1,0:T(8,128)S(1)} %bitcast.17), kind=kOutput, calls=%fused_computation.19 | convolution fusion | flops 3236691968 | bytes 2621440 | tf_op jit(solution)/shard_map/dot_general | solution.py:58
  70.0 19.5 %fusion.25 = bf16[256,1024]{1,0:T(8,128)(2,1)S(1)} fusion(f32[256,1024]{1,0:T(8,128)S(1)} %fusion.10, f32[256,1024]{1,0:T(8,128)S(1)} %bitcast.15), kind=kOutput, calls=%fused_computation.20 | convolution fusion | flops 3236691968 | bytes 2621440 | tf_op jit(solution)/shard_map/dot_general | solution.py:55
  89.5 1.6 stack.7
  91.1 2.6 stack.8
  93.7 4.5 %fusion.28 = bf16[32,16,16,2,32]{4,0,2,1,3:T(8,128)(2,1)} fusion(bf16[16,16,1,32,32]{4,3,1,0,2:T(8,128)(2,1)} %stack.8, bf16[16,16,1,32,32]{4,3,1,0,2:T(8,128)(2,1)S(1)} %stack.7), kind=kLoop, calls=%fused_computation.23 | loop fusion | flops 524288 | bytes 2097152 | tf_op jit(solution)/shard_map/convert_element_type | solution.py:62
  98.1 8.5 %copy.9 = bf16[32,16,16,2,32]{4,3,2,1,0:T(2,128)(2,1)} copy(bf16[32,16,16,2,32]{4,0,2,1,3:T(8,128)(2,1)} %fusion.28) | data formatting | bytes 2097152 | tf_op jit(solution)/shard_map/convert_element_type | solution.py:62
  106.6 11.7 %convert_element_type.49 = bf16[32,16,1024]{2,1,0:T(8,128)(2,1)} reshape(bf16[32,16,16,2,32]{4,3,2,1,0:T(2,128)(2,1)} %copy.9) | data formatting | bytes 2097152 | tf_op jit(solution)/shard_map/convert_element_type | solution.py:62
  118.4 0.0 copy-start
  118.4 0.0 all-gather.2.cloned.1.call-update
  118.4 2.8 multiply_reduce_fusion
  121.3 261.1 %all-gather.2.cloned.1.call-done = bf16[32,512,1024]{2,1,0:T(8,128)(2,1)} async-done(((bf16[32,16,1024]{2,1,0:T(8,128)(2,1)}), bf16[32,512,1024]{2,1,0:T(8,128)(2,1)}) %all-gather.2.cloned.1.call-update) | async-done | bytes 33554448 | tf_op jit(solution)/shard_map/all_gather | solution.py:73
  382.4 0.0 copy-done
  382.4 15.3 %fusion.46 = (f32[32]{0:T(128)S(1)}, f32[32,16,512]{2,1,0:T(8,128)}) fusion(bf16[32,16,1024]{2,1,0:T(8,128)(2,1)S(1)} %copy-done, bf16[32,512,1024]{2,1,0:T(8,128)(2,1)} %all-gather.2.cloned.1.call-done), kind=kOutput, calls=%fused_computation.45 | convolution fusion | flops 537395200 | bytes 35651712 | tf_op jit(solution)/shard_map/kbj,kcj->kbc/dot_general | solution.py:70
  397.7 15.3 %all_to_all.6 = f32[32,1,32]{2,1,0:T(1,128)S(1)} all-to-all(f32[32,1,32]{2,1,0:T(1,128)S(1)} %broadcast_in_dim.5), channel_id=1, replica_groups=mesh['group'=4,'bl'=32] {'bl'}, dimensions={0} | all-to-all | bytes 8192 | tf_op jit(solution)/shard_map/all_to_all | solution.py:16
  413.0 0.5 broadcast_multiply_fusion.1
  (5 shorter events, 0.1 us)
Async XLA Ops:
  7.2 375.2 %all-gather.2.cloned.1.call-start = ((), (), s32[]{:S(2)}) async-start(), calls=%async_computation.1 | async-start | bytes 34603008 | tf_op jit(solution)/shard_map/all_gather | solution.py:73
  118.4 264.0 %copy-start = (bf16[32,16,1024]{2,1,0:T(8,128)(2,1)S(1)}, bf16[32,16,1024]{2,1,0:T(8,128)(2,1)}, u32[]{:S(2)}) copy-start(bf16[32,16,1024]{2,1,0:T(8,128)(2,1)} %convert_element_type.49) | copy-start | bytes 3145732
Sparse Core Ops, SparseCore 0:
  118.5 263.7 all-gather.1
where the time goes:
time: 421 us; the launch traced here: 420 us
  waiting for transfers between devices  261 us (62%)
  matrix products  94.6 us (22%)
  local copies, waits for them, and re-layouts  24.8 us (6%)
  blocking collectives  15.3 us (4%)
  between operations  14.1 us (3%)
  other arithmetic  10.5 us (2%)
    all_gather x1, waiting for transfers between devices, shards(): lax.all_gather(own, 'bl', axis=1, tiled=True)  261 us
    convert_element_type x2, local copies, waits for them, and re-layouts, delay_spectra(): return stacked.reshape(NF // BW, count, NT * 2 * BW).astype(jnp.bfloat16)  20.2 us
    dot_general x1, matrix products, delay_spectra(): jnp.dot(imag_rows, cosine, precision=high)  20 us
    dot_general x1, matrix products, delay_spectra(): jnp.dot(real_rows, cosine, precision=high)  20 us
    dot_general x1, matrix products, delay_spectra(): jnp.dot(real_rows, sine, precision=high)  19.7 us
    dot_general x1, matrix products, delay_spectra(): jnp.dot(imag_rows, sine, precision=high)  19.5 us
    all_to_all x1, blocking collectives, copy_for_each(): return lax.all_to_all(copies, axis, split_axis=0, concat_axis=0, tiled=True)  15.3 us
    dot_general x1, matrix products, shards(): jnp.einsum('kbj,kcj->kbc', own, lax.all_gather(own, 'bl', axis=1, tiled=T...  15.3 us
  transfers between devices with their start and end apart: 1, of which 1 were waited for; matrix products, arithmetic and copies ran while one was open for 1% of the time, Pallas kernels for 0%

commit v1 on v0

v1 whole, which is shorter than its diff:
```python
import math

import jax
import jax.numpy as jnp
import numpy as np
from jax import lax
from jax.experimental import pallas as pl
from jax.experimental.pallas import tpu as pltpu
from jax.sharding import PartitionSpec as P

NF = 1024
NT = 16
CB = 128
BW = 32
NCB = 8
NB = NF // BW
HALF_ROOT = math.sqrt(0.5)


def taper_table():
    angle = np.arange(NF, dtype=np.float64) * (2.0 * math.pi / (NF - 1))
    taper = 0.35875 - 0.48829 * np.cos(angle) + 0.14128 * np.cos(2.0 * angle) - 0.01168 * np.cos(3.0 * angle)
    return jnp.asarray(taper.astype(np.float32).reshape(NCB, CB))


def transform_tables():
    r = np.arange(8)[:, None, None]
    h = np.arange(128)[None, :, None]
    g = np.arange(CB)[None, None, :]
    phi = ((8 * h + r) * g % NF) * (2.0 * math.pi / NF)
    scale = 1.0 / math.sqrt(NF)
    cosine, sine = np.cos(phi) * scale, np.sin(phi) * scale
    real = np.concatenate([cosine, sine], 2).reshape(8, NB, 1, 4, 2 * CB)
    imag = np.concatenate([-sine, cosine], 2).reshape(8, NB, 1, 4, 2 * CB)
    full = np.concatenate([real, imag], 2).reshape(8, 2 * CB, 2 * CB)
    high = full.astype(jnp.bfloat16)
    low = (full - high.astype(np.float64)).astype(jnp.bfloat16)
    return jnp.asarray(high), jnp.asarray(low)


def fold8(re, im):
    def two(a, b):
        return (a[0] + b[0], a[1] + b[1]), (a[0] - b[0], a[1] - b[1])

    def turn(a):
        return (a[1], -a[0])

    def four(x0, x1, x2, x3):
        s0, d0 = two(x0, x2)
        s1, d1 = two(x1, x3)
        y0, y2 = two(s0, s1)
        d1 = turn(d1)
        y1, y3 = two(d0, d1)
        return y0, y1, y2, y3

    x = list(zip(re, im))
    even = four(x[0], x[2], x[4], x[6])
    odd = four(x[1], x[3], x[5], x[7])
    o1 = odd[1]
    o3 = odd[3]
    w1 = ((o1[0] + o1[1]) * HALF_ROOT, (o1[1] - o1[0]) * HALF_ROOT)
    w3 = ((o3[1] - o3[0]) * HALF_ROOT, -(o3[0] + o3[1]) * HALF_ROOT)
    out = [None] * 8
    for i, o in enumerate((odd[0], w1, turn(odd[2]), w3)):
        out[i], out[i + 4] = two(even[i], o)
    return out


def spectra_kernel(x_hbm, flags_ref, taper_ref, high_ref, low_ref, out_ref, xs, yh, yl, z, sems):
    copies = [
        pltpu.make_async_copy(x_hbm.at[part, :, t, :], xs.at[part, t], sems.at[part, t])
        for t in range(NT)
        for part in range(2)
    ]
    for c in copies:
        c.start()
    rows = flags_ref.shape[0]
    weight = []
    for a in range(NCB):
        keep = jnp.broadcast_to(flags_ref[:, a : a + 1].astype(jnp.float32), (rows, CB))
        weight.append(keep * taper_ref[a : a + 1, :])
    for t in range(NT):
        copies[2 * t].wait()
        copies[2 * t + 1].wait()
        parts = [[xs[part, t, :, a * CB : (a + 1) * CB] * weight[a] for a in range(NCB)] for part in range(2)]
        folded = fold8(*parts)
        for r in range(8):
            for part in range(2):
                value = folded[r][part]
                high = value.astype(jnp.bfloat16)
                yh[r, t * rows : (t + 1) * rows, part * CB : (part + 1) * CB] = high
                yl[r, t * rows : (t + 1) * rows, part * CB : (part + 1) * CB] = (
                    value - high.astype(jnp.float32)
                ).astype(jnp.bfloat16)
    dims = (((1,), (1,)), ((), ()))
    for r in range(8):
        z[r] = (
            lax.dot_general(high_ref[r], yh[r], dims, preferred_element_type=jnp.float32)
            + lax.dot_general(low_ref[r], yh[r], dims, preferred_element_type=jnp.float32)
            + lax.dot_general(high_ref[r], yl[r], dims, preferred_element_type=jnp.float32)
        )
    for k in range(NB):
        lower = z[:, 8 * k : 8 * k + 8, 0:128].reshape(64, 128)
        upper = z[:, 8 * k : 8 * k + 8, 128:256].reshape(64, 128)
        block = jnp.concatenate([lower, upper], 0).T.astype(jnp.bfloat16)
        for i in range(8):
            out_ref[k, :, i * 128 : (i + 1) * 128] = block[i * rows : (i + 1) * rows, :]


def spectra(visibilities, flags):
    rows = visibilities.shape[1]
    high, low = transform_tables()
    vmem = pl.BlockSpec(memory_space=pltpu.VMEM)
    return pl.pallas_call(
        spectra_kernel,
        out_shape=jax.ShapeDtypeStruct((NB, rows, NT * 2 * BW), jnp.bfloat16),
        in_specs=[pl.BlockSpec(memory_space=pl.ANY), vmem, vmem, vmem, vmem],
        out_specs=vmem,
        scratch_shapes=[
            pltpu.VMEM((2, NT, rows, NF), jnp.float32),
            pltpu.VMEM((8, NT * rows, 2 * CB), jnp.bfloat16),
            pltpu.VMEM((8, NT * rows, 2 * CB), jnp.bfloat16),
            pltpu.VMEM((8, 2 * CB, NT * rows), jnp.float32),
            pltpu.SemaphoreType.DMA((2, NT)),
        ],
        name="spectra",
    )(visibilities, flags, taper_table(), high, low)


def cross_kernel(own_ref, out_ref):
    count = out_ref.shape[0]
    rows = out_ref.shape[1]
    total = count * rows
    delayed = own_ref[...].reshape(total, own_ref.shape[2])
    power = lax.dot_general(
        delayed, delayed, (((1,), (1,)), ((), ())), preferred_element_type=jnp.float32
    ) * (1.0 / NT)
    out_ref[:, :, 0:total] = power.astype(jnp.bfloat16).reshape(count, rows, total)
    row = lax.broadcasted_iota(jnp.int32, (total, total), 0)
    col = lax.broadcasted_iota(jnp.int32, (total, total), 1)
    off = jnp.where(row == col, 0.0, power)
    band = jnp.sum(jnp.sum(off, axis=0, keepdims=True), axis=1, keepdims=True) * (1.0 / total)
    band = jnp.broadcast_to(band, (rows, 128))
    first = band.astype(jnp.bfloat16).astype(jnp.float32)
    second = (band - first).astype(jnp.bfloat16).astype(jnp.float32)
    third = band - first - second
    lane = lax.broadcasted_iota(jnp.int32, (rows, 128), 1)
    tail = jnp.where(lane == 0, first, jnp.where(lane == 1, second, jnp.where(lane == 2, third, 0.0)))
    tail = tail.astype(jnp.bfloat16)
    for s in range(count):
        out_ref[s, :, total : total + 128] = tail


def cross(delayed):
    count, rows, _ = delayed.shape
    vmem = pl.BlockSpec(memory_space=pltpu.VMEM)
    return pl.pallas_call(
        cross_kernel,
        out_shape=jax.ShapeDtypeStruct((count, rows, count * rows + 128), jnp.bfloat16),
        in_specs=[vmem],
        out_specs=vmem,
        name="cross",
    )(delayed)


def shards(visibilities, flags):
    own = spectra(visibilities, flags)
    mine = lax.all_to_all(own, "bl", 0, 0, tiled=True)
    back = lax.all_to_all(cross(mine), "bl", 0, 0, tiled=True)
    total = back.shape[2] - 128
    power = back[:, :, :total].astype(jnp.float32)
    band = jnp.sum(back[:, 0, total : total + 3].astype(jnp.float32), axis=1)
    return (power, band)


def solution(mesh):
    return jax.shard_map(
        shards,
        mesh=mesh,
        in_specs=(P(None, ("group", "bl"), None, None), P(("group", "bl"), None)),
        out_specs=(P(None, ("group", "bl"), None), P("group")),
        check_vma=False,
    )
```

time: 421 us -> 60.6 us (0.14)
  waiting for transfers between devices: 261 us -> 0 us
  matrix products: 94.6 us -> 0 us
  blocking collectives: 15.3 us -> 47.3 us
  local copies, waits for them, and re-layouts: 24.8 us -> 1.35 us
  between operations: 14.1 us -> 0.64 us
  Pallas kernels: 0 us -> 8.85 us
  other arithmetic: 10.5 us -> 1.93 us
    all_gather x1 -> x0, waiting for transfers between devices: 261 us -> none  [shards(): lax.all_gather(own, 'bl', axis=1, tiled=True)]
    dot_general x5 -> x0, matrix products: 94.6 us -> none  [the longest x1 20 us: delay_spectra(): jnp.dot(imag_rows, cosine, precision=high)]
    all_to_all x1 -> x2, blocking collectives: 15.3 us -> 47.3 us  [the longest x1 28.9 us: shards(): mine = lax.all_to_all(own, 'bl', 0, 0, tiled=True)]
    convert_element_type x3 -> x0, local copies, waits for them, and re-layouts: 20.3 us -> none  [the longest x2 20.2 us: delay_spectra(): return stacked.reshape(NF // BW, count, NT * 2 * BW).astype(jnp.bfloat16)]
    pallas_call x0 -> x2, Pallas kernels: none -> 8.85 us  [the longest x1 5.94 us: spectra(): pl.pallas_call(spectra_kernel, out_shape=jax.ShapeDtypeStruct((NB, rows,...]
  transfers between devices with their start and end apart: 1 -> 0, of which waited for: 1 -> 0; matrix products, arithmetic and copies ran while one was open for 1% -> 0% of each run, Pallas kernels for 0% -> 0%
where the time goes in v1:
time: 60.6 us; the launch traced here: 60.1 us
  blocking collectives  47.3 us (78%)
  Pallas kernels  8.85 us (15%)
  other arithmetic  1.93 us (3%)
  local copies, waits for them, and re-layouts  1.35 us (2%)
  between operations  0.64 us (1%)
    all_to_all x1, blocking collectives, shards(): mine = lax.all_to_all(own, 'bl', 0, 0, tiled=True)  28.9 us
    all_to_all x1, blocking collectives, shards(): back = lax.all_to_all(cross(mine), 'bl', 0, 0, tiled=True)  18.4 us
    pallas_call x1, Pallas kernels, spectra(): pl.pallas_call(spectra_kernel, out_shape=jax.ShapeDtypeStruct((NB, rows,...  5.94 us
    pallas_call x1, Pallas kernels, cross(): pl.pallas_call(cross_kernel, out_shape=jax.ShapeDtypeStruct((count, rows,...  2.91 us
    unnamed x1, local copies, waits for them, and re-layouts  1.35 us

profile of v1, /device:TPU:0, one launch (start us, length us, event | category | flops | bytes accessed | tf_op | source)
XLA Modules:
  0.0 60.1 jit_solution(28228535868561493)
XLA Ops:
  0.6 1.4 %copy.7.flags_ref = s32[16,8]{1,0:T(8,128)} copy(s32[16,8]{0,1:T(8,128)} %param.6) | data formatting | bytes 1024 | tf_op args[1]
  2.0 5.9 %spectra.1 = bf16[32,16,1024]{2,1,0:T(8,128)(2,1)} custom-call(f32[2,16,16,1024]{3,2,1,0:T(8,128)} %x_hbm.1, s32[16,8]{1,0:T(8,128)} %copy.7.flags_ref, f32[8,128]{1,0:T(8,128)} %constant.10.clone.taper_ref, bf16[8,256,256]{2,1,0:T(8,128)(2,1)} %constant.8.clone.high_ref, bf16[8,256,256]{2,1,0:T(8,128)(2,1)} %constant.9.clone.low_ref), custom_call_target="tpu_custom_call" | custom-call | tf_op jit(solution)/shard_map/spectra/pallas_call | solution.py:114
  7.9 28.9 %all_to_all.10.own_ref = bf16[32,16,1024]{2,1,0:T(8,128)(2,1)} all-to-all(bf16[32,16,1024]{2,1,0:T(8,128)(2,1)} %spectra.1), channel_id=1, replica_groups=mesh['group'=4,'bl'=32] {'bl'}, dimensions={0} | all-to-all | bytes 2097152 | tf_op jit(solution)/shard_map/all_to_all | solution.py:168
  36.9 2.9 %cross.1 = bf16[32,16,640]{2,1,0:T(8,128)(2,1)} custom-call(bf16[32,16,1024]{2,1,0:T(8,128)(2,1)} %all_to_all.10.own_ref), custom_call_target="tpu_custom_call" | custom-call | tf_op jit(solution)/shard_map/cross/pallas_call | solution.py:157
  39.8 18.4 %all_to_all.11 = bf16[32,16,640]{2,1,0:T(8,128)(2,1)S(1)} all-to-all(bf16[32,16,640]{2,1,0:T(8,128)(2,1)} %cross.1), channel_id=1, replica_groups=mesh['group'=4,'bl'=32] {'bl'}, dimensions={0} | all-to-all | bytes 1310720 | tf_op jit(solution)/shard_map/all_to_all | solution.py:169
  58.1 0.8 %fusion = f32[32]{0:T(128)} fusion(bf16[32,16,640]{2,1,0:T(8,128)(2,1)S(1)} %all_to_all.11), kind=kLoop, calls=%fused_computation.2 | loop fusion | flops 160 | bytes 320 | tf_op jit(solution)/shard_map/reduce_sum | solution.py:172
  59.0 1.1 %slice_convert_fusion = f32[32,16,512]{2,1,0:T(8,128)} fusion(bf16[32,16,640]{2,1,0:T(8,128)(2,1)S(1)} %all_to_all.11), kind=kLoop, calls=%fused_computation | loop fusion | flops 262144 | bytes 1572864 | tf_op jit(solution)/shard_map/convert_element_type | solution.py:171

commit v2 on v1

--- a/solution.py
+++ b/solution.py
@@ -66,7 +66,7 @@
     return out
 
 
-def spectra_kernel(x_hbm, flags_ref, taper_ref, high_ref, low_ref, out_ref, xs, yh, yl, z, sems):
+def spectra_kernel(x_hbm, flags_ref, taper_ref, high_hbm, low_hbm, out_hbm, xs, yh, yl, z, high_ref, low_ref, out_ref, sems, table_sems, out_sems):
     copies = [
         pltpu.make_async_copy(x_hbm.at[part, :, t, :], xs.at[part, t], sems.at[part, t])
         for t in range(NT)
@@ -74,10 +74,17 @@
     ]
     for c in copies:
         c.start()
-    rows = flags_ref.shape[0]
+    tables = [
+        pltpu.make_async_copy(high_hbm, high_ref, table_sems.at[0]),
+        pltpu.make_async_copy(low_hbm, low_ref, table_sems.at[1]),
+    ]
+    for c in tables:
+        c.start()
+    rows = flags_ref.shape[1]
+    flags = flags_ref[...].astype(jnp.float32).T
     weight = []
     for a in range(NCB):
-        keep = jnp.broadcast_to(flags_ref[:, a : a + 1].astype(jnp.float32), (rows, CB))
+        keep = jnp.broadcast_to(flags[:, a : a + 1], (rows, CB))
         weight.append(keep * taper_ref[a : a + 1, :])
     for t in range(NT):
         copies[2 * t].wait()
@@ -92,6 +99,8 @@
                 yl[r, t * rows : (t + 1) * rows, part * CB : (part + 1) * CB] = (
                     value - high.astype(jnp.float32)
                 ).astype(jnp.bfloat16)
+    for c in tables:
+        c.wait()
     dims = (((1,), (1,)), ((), ()))
     for r in range(8):
         z[r] = (
@@ -99,37 +108,50 @@
             + lax.dot_general(low_ref[r], yh[r], dims, preferred_element_type=jnp.float32)
             + lax.dot_general(high_ref[r], yl[r], dims, preferred_element_type=jnp.float32)
         )
+    sends = []
     for k in range(NB):
         lower = z[:, 8 * k : 8 * k + 8, 0:128].reshape(64, 128)
         upper = z[:, 8 * k : 8 * k + 8, 128:256].reshape(64, 128)
         block = jnp.concatenate([lower, upper], 0).T.astype(jnp.bfloat16)
         for i in range(8):
             out_ref[k, :, i * 128 : (i + 1) * 128] = block[i * rows : (i + 1) * rows, :]
+        if k % 8 == 7:
+            part = pl.ds(k - 7, 8)
+            sends.append(pltpu.make_async_copy(out_ref.at[part], out_hbm.at[part], out_sems.at[k // 8]))
+            sends[-1].start()
+    for c in sends:
+        c.wait()
 
 
 def spectra(visibilities, flags):
     rows = visibilities.shape[1]
     high, low = transform_tables()
     vmem = pl.BlockSpec(memory_space=pltpu.VMEM)
+    hbm = pl.BlockSpec(memory_space=pltpu.HBM)
     return pl.pallas_call(
         spectra_kernel,
         out_shape=jax.ShapeDtypeStruct((NB, rows, NT * 2 * BW), jnp.bfloat16),
-        in_specs=[pl.BlockSpec(memory_space=pl.ANY), vmem, vmem, vmem, vmem],
-        out_specs=vmem,
+        in_specs=[hbm, vmem, vmem, hbm, hbm],
+        out_specs=hbm,
+        compiler_params=pltpu.CompilerParams(vmem_limit_bytes=63 << 20),
         scratch_shapes=[
             pltpu.VMEM((2, NT, rows, NF), jnp.float32),
             pltpu.VMEM((8, NT * rows, 2 * CB), jnp.bfloat16),
             pltpu.VMEM((8, NT * rows, 2 * CB), jnp.bfloat16),
             pltpu.VMEM((8, 2 * CB, NT * rows), jnp.float32),
+            pltpu.VMEM(high.shape, jnp.bfloat16),
+            pltpu.VMEM(low.shape, jnp.bfloat16),
+            pltpu.VMEM((NB, rows, NT * 2 * BW), jnp.bfloat16),
             pltpu.SemaphoreType.DMA((2, NT)),
+            pltpu.SemaphoreType.DMA((2,)),
+            pltpu.SemaphoreType.DMA((NB // 8,)),
         ],
         name="spectra",
-    )(visibilities, flags, taper_table(), high, low)
+    )(visibilities, flags.T, taper_table(), high, low)
 
 
 def cross_kernel(own_ref, out_ref):
-    count = out_ref.shape[0]
-    rows = out_ref.shape[1]
+    count, rows, _ = out_ref.shape
     total = count * rows
     delayed = own_ref[...].reshape(total, own_ref.shape[2])
     power = lax.dot_general(
@@ -140,15 +162,17 @@
     col = lax.broadcasted_iota(jnp.int32, (total, total), 1)
     off = jnp.where(row == col, 0.0, power)
     band = jnp.sum(jnp.sum(off, axis=0, keepdims=True), axis=1, keepdims=True) * (1.0 / total)
-    band = jnp.broadcast_to(band, (rows, 128))
+    band = jnp.broadcast_to(band, (rows, total))
     first = band.astype(jnp.bfloat16).astype(jnp.float32)
     second = (band - first).astype(jnp.bfloat16).astype(jnp.float32)
     third = band - first - second
-    lane = lax.broadcasted_iota(jnp.int32, (rows, 128), 1)
-    tail = jnp.where(lane == 0, first, jnp.where(lane == 1, second, jnp.where(lane == 2, third, 0.0)))
-    tail = tail.astype(jnp.bfloat16)
+    row = lax.broadcasted_iota(jnp.int32, (rows, total), 0)
+    col = lax.broadcasted_iota(jnp.int32, (rows, total), 1)
+    term = jnp.where(row == 1, first, jnp.where(row == 2, second, third))
+    spare = (row >= 1) & (row <= 3)
     for s in range(count):
-        out_ref[s, :, total : total + 128] = tail
+        piece = power[s * rows : (s + 1) * rows]
+        out_ref[s] = jnp.where(spare & (col == s * rows), term, piece).astype(jnp.bfloat16)
 
 
 def cross(delayed):
@@ -156,21 +180,54 @@
     vmem = pl.BlockSpec(memory_space=pltpu.VMEM)
     return pl.pallas_call(
         cross_kernel,
-        out_shape=jax.ShapeDtypeStruct((count, rows, count * rows + 128), jnp.bfloat16),
+        out_shape=jax.ShapeDtypeStruct((count, rows, count * rows), jnp.bfloat16),
         in_specs=[vmem],
         out_specs=vmem,
+        compiler_params=pltpu.CompilerParams(vmem_limit_bytes=8 << 20),
         name="cross",
     )(delayed)
+
+
+def finish_kernel(back_ref, power_ref, band_ref):
+    bands, rows, total = back_ref.shape
+    start = lax.axis_index("bl") * rows
+    power = back_ref[...].astype(jnp.float32)
+    power_ref[...] = power
+    lane = lax.broadcasted_iota(jnp.int32, (bands, total), 1)
+    top = power[:, 0, :]
+    band = jnp.zeros((bands, 1), jnp.float32)
+    for i in range(1, 4):
+        line = power[:, i, :]
+        band += jnp.sum(jnp.where(lane == start, line, 0.0), axis=1, keepdims=True)
+        value = jnp.sum(jnp.where(lane == start + i, top, 0.0), axis=1, keepdims=True)
+        power_ref[:, i, :] = jnp.where(lane == start, value, line)
+    row = lax.broadcasted_iota(jnp.int32, (bands, bands), 0)
+    col = lax.broadcasted_iota(jnp.int32, (bands, bands), 1)
+    band_ref[...] = jnp.sum(jnp.where(row == col, band, 0.0), axis=0, keepdims=True)
+
+
+def finish(back):
+    bands, rows, total = back.shape
+    vmem = pl.BlockSpec(memory_space=pltpu.VMEM)
+    return pl.pallas_call(
+        finish_kernel,
+        out_shape=(
+            jax.ShapeDtypeStruct((bands, rows, total), jnp.float32),
+            jax.ShapeDtypeStruct((1, bands), jnp.float32),
+        ),
+        in_specs=[vmem],
+        out_specs=(vmem, vmem),
+        compiler_params=pltpu.CompilerParams(vmem_limit_bytes=8 << 20),
+        name="finish",
+    )(back)
 
 
 def shards(visibilities, flags):
     own = spectra(visibilities, flags)
     mine = lax.all_to_all(own, "bl", 0, 0, tiled=True)
     back = lax.all_to_all(cross(mine), "bl", 0, 0, tiled=True)
-    total = back.shape[2] - 128
-    power = back[:, :, :total].astype(jnp.float32)
-    band = jnp.sum(back[:, 0, total : total + 3].astype(jnp.float32), axis=1)
-    return (power, band)
+    power, band = finish(back)
+    return (power, band.reshape(-1))
 
 
 def solution(mesh):

time: 60.6 us -> 54.5 us (0.90)
  other arithmetic: 1.93 us -> 0 us
  blocking collectives: 47.3 us -> 45.8 us
  local copies, waits for them, and re-layouts: 1.35 us -> 0 us
  Pallas kernels: 8.85 us -> 7.76 us
    pallas_call x1, Pallas kernels: 2.91 us -> 0.86 us  [cross(): pl.pallas_call(cross_kernel, out_shape=jax.ShapeDtypeStruct((count, rows,...]
    all_to_all x1, blocking collectives: 18.4 us -> 16.9 us  [shards(): back = lax.all_to_all(cross(mine), 'bl', 0, 0, tiled=True)]
    unnamed x1 -> x0, local copies, waits for them, and re-layouts: 1.35 us -> none
    pallas_call x0 -> x1, Pallas kernels: none -> 1.25 us  [finish(): pl.pallas_call(finish_kernel, out_shape=(jax.ShapeDtypeStruct((bands, row...]
    convert_element_type x1 -> x0, other arithmetic: 1.1 us -> none  [shards(): power = back[:, :, :total].astype(jnp.float32)]
    reduce_sum x1 -> x0, other arithmetic: 0.83 us -> none  [shards(): band = jnp.sum(back[:, 0, total:total + 3].astype(jnp.float32), axis=1)]
where the time goes in v2:
time: 54.5 us; the launch traced here: 54.2 us
  blocking collectives  45.8 us (84%)
  Pallas kernels  7.76 us (14%)
  between operations  0.65 us (1%)
    all_to_all x1, blocking collectives, shards(): mine = lax.all_to_all(own, 'bl', 0, 0, tiled=True)  28.8 us
    all_to_all x1, blocking collectives, shards(): back = lax.all_to_all(cross(mine), 'bl', 0, 0, tiled=True)  16.9 us
    pallas_call x1, Pallas kernels, spectra(): pl.pallas_call(spectra_kernel, out_shape=jax.ShapeDtypeStruct((NB, rows,...  5.64 us
    pallas_call x1, Pallas kernels, finish(): pl.pallas_call(finish_kernel, out_shape=(jax.ShapeDtypeStruct((bands, row...  1.25 us

profile of v2, /device:TPU:0, one launch (start us, length us, event | category | flops | bytes accessed | tf_op | source)
XLA Modules:
  0.0 54.2 jit_solution(6216973304629114426)
XLA Ops:
  0.6 5.6 %spectra.1 = bf16[32,16,1024]{2,1,0:T(8,128)(2,1)} custom-call(f32[2,16,16,1024]{3,2,1,0:T(8,128)} %x_hbm.1, s32[8,16]{1,0:T(8,128)} %bitcast.2, f32[8,128]{1,0:T(8,128)} %constant.8.clone.taper_ref, bf16[8,256,256]{2,1,0:T(8,128)(2,1)} %constant.6.clone.high_hbm, bf16[8,256,256]{2,1,0:T(8,128)(2,1)} %constant.7.clone.low_hbm), custom_call_target="tpu_custom_call" | custom-call | tf_op jit(solution)/shard_map/spectra/pallas_call | solution.py:131
  6.3 28.8 %all_to_all.10.own_ref = bf16[32,16,1024]{2,1,0:T(8,128)(2,1)S(1)} all-to-all(bf16[32,16,1024]{2,1,0:T(8,128)(2,1)} %spectra.1), channel_id=1, replica_groups=mesh['group'=4,'bl'=32] {'bl'}, dimensions={0} | all-to-all | bytes 2097152 | tf_op jit(solution)/shard_map/all_to_all | solution.py:227
  35.1 0.9 %cross.1 = bf16[32,16,512]{2,1,0:T(8,128)(2,1)S(1)} custom-call(bf16[32,16,1024]{2,1,0:T(8,128)(2,1)S(1)} %all_to_all.10.own_ref), custom_call_target="tpu_custom_call" | custom-call | tf_op jit(solution)/shard_map/cross/pallas_call | solution.py:181
  36.0 16.9 %all_to_all.11.back_ref = bf16[32,16,512]{2,1,0:T(8,128)(2,1)S(1)} all-to-all(bf16[32,16,512]{2,1,0:T(8,128)(2,1)S(1)} %cross.1), channel_id=1, replica_groups=mesh['group'=4,'bl'=32] {'bl'}, dimensions={0} | all-to-all | bytes 1048576 | tf_op jit(solution)/shard_map/all_to_all | solution.py:228
  52.9 1.3 %finish.1 = (f32[32,16,512]{2,1,0:T(8,128)}, f32[1,32]{1,0:T(1,128)}) custom-call(bf16[32,16,512]{2,1,0:T(8,128)(2,1)S(1)} %all_to_all.11.back_ref), custom_call_target="tpu_custom_call" | custom-call | tf_op jit(solution)/shard_map/finish/pallas_call | solution.py:212

commit v3 on v2

--- a/solution.py
+++ b/solution.py
@@ -24,130 +24,141 @@
 
 
 def transform_tables():
-    r = np.arange(8)[:, None, None]
+    r = np.arange(5)[:, None, None]
     h = np.arange(128)[None, :, None]
     g = np.arange(CB)[None, None, :]
     phi = ((8 * h + r) * g % NF) * (2.0 * math.pi / NF)
     scale = 1.0 / math.sqrt(NF)
     cosine, sine = np.cos(phi) * scale, np.sin(phi) * scale
-    real = np.concatenate([cosine, sine], 2).reshape(8, NB, 1, 4, 2 * CB)
-    imag = np.concatenate([-sine, cosine], 2).reshape(8, NB, 1, 4, 2 * CB)
-    full = np.concatenate([real, imag], 2).reshape(8, 2 * CB, 2 * CB)
+    real = np.concatenate([cosine, sine], 2).reshape(5, NB, 1, 4, 2 * CB)
+    imag = np.concatenate([-sine, cosine], 2).reshape(5, NB, 1, 4, 2 * CB)
+    full = np.concatenate([real, imag], 2).reshape(5, 2 * CB, 2 * CB)
     high = full.astype(jnp.bfloat16)
     low = (full - high.astype(np.float64)).astype(jnp.bfloat16)
-    return jnp.asarray(high), jnp.asarray(low)
-
-
-def fold8(re, im):
-    def two(a, b):
-        return (a[0] + b[0], a[1] + b[1]), (a[0] - b[0], a[1] - b[1])
-
-    def turn(a):
-        return (a[1], -a[0])
-
-    def four(x0, x1, x2, x3):
-        s0, d0 = two(x0, x2)
-        s1, d1 = two(x1, x3)
-        y0, y2 = two(s0, s1)
-        d1 = turn(d1)
-        y1, y3 = two(d0, d1)
-        return y0, y1, y2, y3
-
-    x = list(zip(re, im))
-    even = four(x[0], x[2], x[4], x[6])
-    odd = four(x[1], x[3], x[5], x[7])
-    o1 = odd[1]
-    o3 = odd[3]
-    w1 = ((o1[0] + o1[1]) * HALF_ROOT, (o1[1] - o1[0]) * HALF_ROOT)
-    w3 = ((o3[1] - o3[0]) * HALF_ROOT, -(o3[0] + o3[1]) * HALF_ROOT)
-    out = [None] * 8
-    for i, o in enumerate((odd[0], w1, turn(odd[2]), w3)):
-        out[i], out[i + 4] = two(even[i], o)
-    return out
-
-
-def spectra_kernel(x_hbm, flags_ref, taper_ref, high_hbm, low_hbm, out_hbm, xs, yh, yl, z, high_ref, low_ref, out_ref, sems, table_sems, out_sems):
+    return jnp.asarray(np.stack([high, low], 1))
+
+
+def two(a, b):
+    return (a[0] + b[0], a[1] + b[1]), (a[0] - b[0], a[1] - b[1])
+
+
+def four(x0, x1, x2, x3, conjugated):
+    s0, d0 = two(x0, x2)
+    s1, d1 = two(x1, x3)
+    d1 = (d1[1], -d1[0])
+    y = [*two(s0, s1), *two(d0, d1)]
+    y = [y[0], y[2], y[1], y[3]]
+    minus = {2: (s1, s0), 3: (d1, d0)}
+    for i in conjugated:
+        y[i] = (y[i][0], minus[i][0][1] - minus[i][1][1])
+    return y
+
+
+def split_store(value, high_ref, low_ref, r, row, part):
+    high = value.astype(jnp.bfloat16)
+    at = (r, pl.ds(row, value.shape[0]), pl.ds(part * CB, CB))
+    high_ref[at] = high
+    low_ref[at] = (value - high.astype(jnp.float32)).astype(jnp.bfloat16)
+
+
+def spectra_kernel(
+    x_hbm, flags_hbm, taper_hbm, table_hbm, out_ref, xs, flags_ref, taper_ref, yh, yl, z, table, sems, side_sems
+):
+    rows = flags_ref.shape[1]
+    small = [
+        pltpu.make_async_copy(flags_hbm, flags_ref, side_sems.at[0]),
+        pltpu.make_async_copy(taper_hbm, taper_ref, side_sems.at[1]),
+    ]
     copies = [
         pltpu.make_async_copy(x_hbm.at[part, :, t, :], xs.at[part, t], sems.at[part, t])
         for t in range(NT)
         for part in range(2)
     ]
-    for c in copies:
+    tables = pltpu.make_async_copy(table_hbm, table, side_sems.at[2])
+    for c in [*small, tables, *copies]:
         c.start()
-    tables = [
-        pltpu.make_async_copy(high_hbm, high_ref, table_sems.at[0]),
-        pltpu.make_async_copy(low_hbm, low_ref, table_sems.at[1]),
-    ]
-    for c in tables:
-        c.start()
-    rows = flags_ref.shape[1]
+    for c in small:
+        c.wait()
     flags = flags_ref[...].astype(jnp.float32).T
     weight = []
     for a in range(NCB):
         keep = jnp.broadcast_to(flags[:, a : a + 1], (rows, CB))
         weight.append(keep * taper_ref[a : a + 1, :])
+
+    def lanes(a):
+        return slice(a * CB, (a + 1) * CB)
+
+    def multiply(r):
+        dims = (((1,), (1,)), ((), ()))
+        i = min(r, 8 - r)
+        z[r] = (
+            lax.dot_general(table[i, 0], yh[r], dims, preferred_element_type=jnp.float32)
+            + lax.dot_general(table[i, 1], yh[r], dims, preferred_element_type=jnp.float32)
+            + lax.dot_general(table[i, 0], yl[r], dims, preferred_element_type=jnp.float32)
+        )
+
     for t in range(NT):
         copies[2 * t].wait()
         copies[2 * t + 1].wait()
-        parts = [[xs[part, t, :, a * CB : (a + 1) * CB] * weight[a] for a in range(NCB)] for part in range(2)]
-        folded = fold8(*parts)
-        for r in range(8):
+        u = [tuple(xs[part, t, :, lanes(a)] * weight[a] for part in range(2)) for a in range(NCB)]
+        pairs = [two(u[a], u[a + 4]) for a in range(4)]
+        for a in range(4):
             for part in range(2):
-                value = folded[r][part]
-                high = value.astype(jnp.bfloat16)
-                yh[r, t * rows : (t + 1) * rows, part * CB : (part + 1) * CB] = high
-                yl[r, t * rows : (t + 1) * rows, part * CB : (part + 1) * CB] = (
-                    value - high.astype(jnp.float32)
-                ).astype(jnp.bfloat16)
-    for c in tables:
-        c.wait()
-    dims = (((1,), (1,)), ((), ()))
-    for r in range(8):
-        z[r] = (
-            lax.dot_general(high_ref[r], yh[r], dims, preferred_element_type=jnp.float32)
-            + lax.dot_general(low_ref[r], yh[r], dims, preferred_element_type=jnp.float32)
-            + lax.dot_general(high_ref[r], yl[r], dims, preferred_element_type=jnp.float32)
-        )
-    sends = []
+                xs[part, t, :, lanes(a)] = pairs[a][1][part]
+        y = four(*(p[0] for p in pairs), conjugated=(3,))
+        for m in range(4):
+            for part in range(2):
+                split_store(y[m][part], yh, yl, 2 * m, t * rows, part)
+    tables.wait()
+    for t in range(NT):
+        if t % 4 == 0:
+            multiply((0, 4, 2, 6)[t // 4])
+        d = [tuple(xs[part, t, :, lanes(a)] for part in range(2)) for a in range(4)]
+        d[1] = ((d[1][0] + d[1][1]) * HALF_ROOT, (d[1][1] - d[1][0]) * HALF_ROOT)
+        d[2] = (d[2][1], -d[2][0])
+        d[3] = ((d[3][1] - d[3][0]) * HALF_ROOT, (d[3][0] + d[3][1]) * -HALF_ROOT)
+        y = four(*d, conjugated=(2, 3))
+        for m in range(4):
+            for part in range(2):
+                split_store(y[m][part], yh, yl, 2 * m + 1, t * rows, part)
+    for r in (1, 7, 3, 5):
+        multiply(r)
     for k in range(NB):
-        lower = z[:, 8 * k : 8 * k + 8, 0:128].reshape(64, 128)
-        upper = z[:, 8 * k : 8 * k + 8, 128:256].reshape(64, 128)
+        straight, turned = pl.ds(8 * k, 8), pl.ds(8 * (NB - 1 - k), 8)
+        lower = jnp.concatenate([z[r, straight if r < 5 else turned, 0:128] for r in range(8)], 0)
+        upper = jnp.concatenate([z[r, straight if r < 5 else turned, 128:256] for r in range(8)], 0)
         block = jnp.concatenate([lower, upper], 0).T.astype(jnp.bfloat16)
         for i in range(8):
             out_ref[k, :, i * 128 : (i + 1) * 128] = block[i * rows : (i + 1) * rows, :]
-        if k % 8 == 7:
-            part = pl.ds(k - 7, 8)
-            sends.append(pltpu.make_async_copy(out_ref.at[part], out_hbm.at[part], out_sems.at[k // 8]))
-            sends[-1].start()
-    for c in sends:
-        c.wait()
+
+
+def in_hbm(array):
+    return pltpu.with_memory_space_constraint(array, pltpu.HBM)
 
 
 def spectra(visibilities, flags):
     rows = visibilities.shape[1]
-    high, low = transform_tables()
-    vmem = pl.BlockSpec(memory_space=pltpu.VMEM)
+    table = transform_tables()
     hbm = pl.BlockSpec(memory_space=pltpu.HBM)
     return pl.pallas_call(
         spectra_kernel,
-        out_shape=jax.ShapeDtypeStruct((NB, rows, NT * 2 * BW), jnp.bfloat16),
-        in_specs=[hbm, vmem, vmem, hbm, hbm],
-        out_specs=hbm,
-        compiler_params=pltpu.CompilerParams(vmem_limit_bytes=63 << 20),
+        out_shape=pltpu.VMEM((NB, rows, NT * 2 * BW), jnp.bfloat16),
+        in_specs=[hbm] * 4,
+        out_specs=pl.BlockSpec(memory_space=pltpu.VMEM),
+        compiler_params=pltpu.CompilerParams(vmem_limit_bytes=24 << 20),
         scratch_shapes=[
             pltpu.VMEM((2, NT, rows, NF), jnp.float32),
+            pltpu.VMEM((NCB, rows), jnp.int32),
+            pltpu.VMEM((NCB, CB), jnp.float32),
             pltpu.VMEM((8, NT * rows, 2 * CB), jnp.bfloat16),
             pltpu.VMEM((8, NT * rows, 2 * CB), jnp.bfloat16),
             pltpu.VMEM((8, 2 * CB, NT * rows), jnp.float32),
-            pltpu.VMEM(high.shape, jnp.bfloat16),
-            pltpu.VMEM(low.shape, jnp.bfloat16),
-            pltpu.VMEM((NB, rows, NT * 2 * BW), jnp.bfloat16),
+            pltpu.VMEM(table.shape, jnp.bfloat16),
             pltpu.SemaphoreType.DMA((2, NT)),
-            pltpu.SemaphoreType.DMA((2,)),
-            pltpu.SemaphoreType.DMA((NB // 8,)),
+            pltpu.SemaphoreType.DMA((3,)),
         ],
         name="spectra",
-    )(visibilities, flags.T, taper_table(), high, low)
+    )(in_hbm(visibilities), in_hbm(flags.T), in_hbm(taper_table()), in_hbm(table))
 
 
 def cross_kernel(own_ref, out_ref):

time: 54.5 us -> 52.4 us (0.961)
  Pallas kernels: 7.76 us -> 6 us
    pallas_call x1, Pallas kernels: 5.64 us -> 3.88 us  [spectra(): pl.pallas_call(spectra_kernel, out_shape=pltpu.VMEM((NB, rows, NT * 2 * B...]
where the time goes in v3:
time: 52.4 us; the launch traced here: 52.2 us
  blocking collectives  45.5 us (87%)
  Pallas kernels  6 us (11%)
  between operations  0.65 us (1%)
    all_to_all x1, blocking collectives, shards(): mine = lax.all_to_all(own, 'bl', 0, 0, tiled=True)  28.6 us
    all_to_all x1, blocking collectives, shards(): back = lax.all_to_all(cross(mine), 'bl', 0, 0, tiled=True)  16.9 us
    pallas_call x1, Pallas kernels, spectra(): pl.pallas_call(spectra_kernel, out_shape=pltpu.VMEM((NB, rows, NT * 2 * B...  3.88 us
    pallas_call x1, Pallas kernels, finish(): pl.pallas_call(finish_kernel, out_shape=(jax.ShapeDtypeStruct((bands, row...  1.25 us

profile of v3, /device:TPU:0, one launch (start us, length us, event | category | flops | bytes accessed | tf_op | source)
XLA Modules:
  0.0 52.2 jit_solution(5775618890734314541)
XLA Ops:
  0.6 3.9 %spectra.1 = bf16[32,16,1024]{2,1,0:T(8,128)(2,1)S(1)} custom-call(f32[2,16,16,1024]{3,2,1,0:T(8,128)} %x_hbm.1, s32[8,16]{1,0:T(8,128)} %bitcast.2, f32[8,128]{1,0:T(8,128)} %constant.5.clone.taper_hbm, bf16[5,2,256,256]{3,2,1,0:T(8,128)(2,1)} %constant.4.clone.table_hbm), custom_call_target="tpu_custom_call" | custom-call | tf_op jit(solution)/shard_map/spectra/pallas_call | solution.py:143
  4.5 28.6 %all_to_all.10.own_ref = bf16[32,16,1024]{2,1,0:T(8,128)(2,1)S(1)} all-to-all(bf16[32,16,1024]{2,1,0:T(8,128)(2,1)S(1)} %spectra.1), channel_id=1, replica_groups=mesh['group'=4,'bl'=32] {'bl'}, dimensions={0} | all-to-all | bytes 2097152 | tf_op jit(solution)/shard_map/all_to_all | solution.py:238
  33.1 0.9 %cross.1 = bf16[32,16,512]{2,1,0:T(8,128)(2,1)S(1)} custom-call(bf16[32,16,1024]{2,1,0:T(8,128)(2,1)S(1)} %all_to_all.10.own_ref), custom_call_target="tpu_custom_call" | custom-call | tf_op jit(solution)/shard_map/cross/pallas_call | solution.py:192
  34.0 16.9 %all_to_all.11.back_ref = bf16[32,16,512]{2,1,0:T(8,128)(2,1)S(1)} all-to-all(bf16[32,16,512]{2,1,0:T(8,128)(2,1)S(1)} %cross.1), channel_id=1, replica_groups=mesh['group'=4,'bl'=32] {'bl'}, dimensions={0} | all-to-all | bytes 1048576 | tf_op jit(solution)/shard_map/all_to_all | solution.py:239
  50.9 1.3 %finish.1 = (f32[32,16,512]{2,1,0:T(8,128)}, f32[1,32]{1,0:T(1,128)}) custom-call(bf16[32,16,512]{2,1,0:T(8,128)(2,1)S(1)} %all_to_all.11.back_ref), custom_call_target="tpu_custom_call" | custom-call | tf_op jit(solution)/shard_map/finish/pallas_call | solution.py:223

commit v4 on v3

v4 whole, which is shorter than its diff:
```python
import math

import jax
import jax.numpy as jnp
import numpy as np
from jax import lax
from jax.experimental import pallas as pl
from jax.experimental.pallas import tpu as pltpu
from jax.sharding import PartitionSpec as P

NF = 1024
NT = 16
CB = 128
BW = 32
NCB = 8
NB = NF // BW
GROUP = 4
HALF_ROOT = math.sqrt(0.5)
OUT = [(-3 * i % 32) ^ 26 for i in range(32)]
BACK = [(-3 * i % 32) ^ 26 for i in range(32)]


def taper_table():
    angle = np.arange(NF, dtype=np.float64) * (2.0 * math.pi / (NF - 1))
    taper = 0.35875 - 0.48829 * np.cos(angle) + 0.14128 * np.cos(2.0 * angle) - 0.01168 * np.cos(3.0 * angle)
    return taper.reshape(NCB, CB)


def transform_table():
    h = np.arange(128)[:, None]
    g = np.arange(CB)[None, :]
    phi = (h * g % CB) * (2.0 * math.pi / CB)
    scale = 1.0 / math.sqrt(NF)
    cosine, sine = np.cos(phi) * scale, np.sin(phi) * scale
    real = np.concatenate([cosine, sine], 1).reshape(NB, 1, 4, 2 * CB)
    imag = np.concatenate([-sine, cosine], 1).reshape(NB, 1, 4, 2 * CB)
    full = np.concatenate([real, imag], 1).reshape(2 * CB, 2 * CB)
    high = full.astype(jnp.bfloat16)
    low = (full - high.astype(np.float64)).astype(jnp.bfloat16)
    return jnp.asarray(np.stack([high, low]))


def row_table():
    phi = np.arange(8)[:, None] * np.arange(CB)[None, :] * (2.0 * math.pi / NF)
    return jnp.asarray(np.concatenate([taper_table(), np.cos(phi), np.sin(phi)]).astype(np.float32))


def two(a, b):
    return (a[0] + b[0], a[1] + b[1]), (a[0] - b[0], a[1] - b[1])


def four(x0, x1, x2, x3):
    s0, d0 = two(x0, x2)
    s1, d1 = two(x1, x3)
    y0, y2 = two(s0, s1)
    y1, y3 = two(d0, (d1[1], -d1[0]))
    return y0, y1, y2, y3


def eight(x):
    pairs = [two(x[a], x[a + 4]) for a in range(4)]
    d = [p[1] for p in pairs]
    d[1] = ((d[1][0] + d[1][1]) * HALF_ROOT, (d[1][1] - d[1][0]) * HALF_ROOT)
    d[2] = (d[2][1], -d[2][0])
    d[3] = ((d[3][1] - d[3][0]) * HALF_ROOT, (d[3][0] + d[3][1]) * -HALF_ROOT)
    even, odd = four(*(p[0] for p in pairs)), four(*d)
    return [even[0], odd[0], even[1], odd[1], even[2], odd[2], even[3], odd[3]]


def spectra_kernel(x_hbm, flags_hbm, rows_hbm, table_hbm, out_ref, xs, flags_ref, rows_ref, yh, yl, z, table, sems, side_sems):
    rows = flags_ref.shape[1]
    small = [
        pltpu.make_async_copy(flags_hbm, flags_ref, side_sems.at[0]),
        pltpu.make_async_copy(rows_hbm, rows_ref, side_sems.at[1]),
    ]
    copies = [
        pltpu.make_async_copy(x_hbm.at[part, :, t, :], xs.at[part, t], sems.at[part, t])
        for t in range(NT)
        for part in range(2)
    ]
    tables = pltpu.make_async_copy(table_hbm, table, side_sems.at[2])
    for c in [*small, tables, *copies]:
        c.start()
    for c in small:
        c.wait()
    flags = flags_ref[...].astype(jnp.float32).T
    weight = []
    for a in range(NCB):
        keep = jnp.broadcast_to(flags[:, a : a + 1], (rows, CB))
        weight.append(keep * rows_ref[a : a + 1, :])

    def fold(t):
        u = [
            tuple(xs[part, t, :, a * CB : (a + 1) * CB] * weight[a] for part in range(2)) for a in range(NCB)
        ]
        y = eight(u)
        for r in range(8):
            re, im = y[r]
            if r:
                cosine, sine = rows_ref[8 + r : 9 + r, :], rows_ref[16 + r : 17 + r, :]
                re, im = re * cosine + im * sine, im * cosine - re * sine
            at = pl.ds((r * GROUP + t % GROUP) * rows, rows)
            for part, value in enumerate((re, im)):
                high = value.astype(jnp.bfloat16)
                yh[t // GROUP, at, part * CB : (part + 1) * CB] = high
                low = (value - high.astype(jnp.float32)).astype(jnp.bfloat16)
                yl[t // GROUP, at, part * CB : (part + 1) * CB] = low

    def multiply(g):
        width = yh.shape[1]
        dims = (((1,), (1,)), ((), ()))
        z[:, g * width : (g + 1) * width] = (
            lax.dot_general(table[0], yh[g], dims, preferred_element_type=jnp.float32)
            + lax.dot_general(table[1], yh[g], dims, preferred_element_type=jnp.float32)
            + lax.dot_general(table[0], yl[g], dims, preferred_element_type=jnp.float32)
        )

    for g in range(NT // GROUP):
        for c in copies[2 * GROUP * g : 2 * GROUP * (g + 1)]:
            c.wait()
        if g == 1:
            tables.wait()
        if g:
            multiply(g - 1)
        for t in range(g * GROUP, (g + 1) * GROUP):
            fold(t)
    multiply(NT // GROUP - 1)
    for k in range(NB):
        tiles = [z[8 * k : 8 * k + 8, m * 128 : (m + 1) * 128] for m in range(z.shape[1] // 128)]
        block = jnp.concatenate(tiles, 0).T.astype(jnp.bfloat16)
        for i in range(8):
            out_ref[k, :, i * 128 : (i + 1) * 128] = block[i * rows : (i + 1) * rows, :]


def in_hbm(array):
    return pltpu.with_memory_space_constraint(array, pltpu.HBM)


def spectra(visibilities, flags):
    rows = visibilities.shape[1]
    table, row = transform_table(), row_table()
    hbm = pl.BlockSpec(memory_space=pltpu.HBM)
    return pl.pallas_call(
        spectra_kernel,
        out_shape=pltpu.VMEM((NB, rows, NT * 2 * BW), jnp.bfloat16),
        in_specs=[hbm] * 4,
        out_specs=pl.BlockSpec(memory_space=pltpu.VMEM),
        compiler_params=pltpu.CompilerParams(vmem_limit_bytes=24 << 20),
        scratch_shapes=[
            pltpu.VMEM((2, NT, rows, NF), jnp.float32),
            pltpu.VMEM((NCB, rows), jnp.int32),
            pltpu.VMEM(row.shape, jnp.float32),
            pltpu.VMEM((NT // GROUP, 8 * GROUP * rows, 2 * CB), jnp.bfloat16),
            pltpu.VMEM((NT // GROUP, 8 * GROUP * rows, 2 * CB), jnp.bfloat16),
            pltpu.VMEM((2 * CB, 8 * NT * rows), jnp.float32),
            pltpu.VMEM(table.shape, jnp.bfloat16),
            pltpu.SemaphoreType.DMA((2, NT)),
            pltpu.SemaphoreType.DMA((3,)),
        ],
        name="spectra",
    )(in_hbm(visibilities), in_hbm(flags.T), in_hbm(row), in_hbm(table))


def cross_kernel(own_ref, out_ref):
    count, rows, _ = out_ref.shape
    total = count * rows
    delayed = jnp.concatenate([own_ref[OUT.index(s)] for s in range(count)], 0)
    power = lax.dot_general(
        delayed, delayed, (((1,), (1,)), ((), ())), preferred_element_type=jnp.float32
    ) * (1.0 / NT)
    out_ref[:, :, 0:total] = power.astype(jnp.bfloat16).reshape(count, rows, total)
    row = lax.broadcasted_iota(jnp.int32, (total, total), 0)
    col = lax.broadcasted_iota(jnp.int32, (total, total), 1)
    off = jnp.where(row == col, 0.0, power)
    band = jnp.sum(jnp.sum(off, axis=0, keepdims=True), axis=1, keepdims=True) * (1.0 / total)
    band = jnp.broadcast_to(band, (rows, total))
    first = band.astype(jnp.bfloat16).astype(jnp.float32)
    second = (band - first).astype(jnp.bfloat16).astype(jnp.float32)
    third = band - first - second
    row = lax.broadcasted_iota(jnp.int32, (rows, total), 0)
    col = lax.broadcasted_iota(jnp.int32, (rows, total), 1)
    term = jnp.where(row == 1, first, jnp.where(row == 2, second, third))
    spare = (row >= 1) & (row <= 3)
    for i, s in enumerate(BACK):
        piece = power[s * rows : (s + 1) * rows]
        out_ref[i] = jnp.where(spare & (col == s * rows), term, piece).astype(jnp.bfloat16)


def cross(delayed):
    count, rows, _ = delayed.shape
    vmem = pl.BlockSpec(memory_space=pltpu.VMEM)
    return pl.pallas_call(
        cross_kernel,
        out_shape=jax.ShapeDtypeStruct((count, rows, count * rows), jnp.bfloat16),
        in_specs=[vmem],
        out_specs=vmem,
        compiler_params=pltpu.CompilerParams(vmem_limit_bytes=8 << 20),
        name="cross",
    )(delayed)


def finish_kernel(back_ref, power_ref, band_ref):
    bands, rows, total = back_ref.shape
    start = lax.axis_index("bl") * rows
    power = jnp.stack([back_ref[BACK.index(s)] for s in OUT]).astype(jnp.float32)
    power_ref[...] = power
    lane = lax.broadcasted_iota(jnp.int32, (bands, total), 1)
    top = power[:, 0, :]
    band = jnp.zeros((bands, 1), jnp.float32)
    for i in range(1, 4):
        line = power[:, i, :]
        band += jnp.sum(jnp.where(lane == start, line, 0.0), axis=1, keepdims=True)
        value = jnp.sum(jnp.where(lane == start + i, top, 0.0), axis=1, keepdims=True)
        power_ref[:, i, :] = jnp.where(lane == start, value, line)
    row = lax.broadcasted_iota(jnp.int32, (bands, bands), 0)
    col = lax.broadcasted_iota(jnp.int32, (bands, bands), 1)
    band_ref[...] = jnp.sum(jnp.where(row == col, band, 0.0), axis=0, keepdims=True)


def finish(back):
    bands, rows, total = back.shape
    vmem = pl.BlockSpec(memory_space=pltpu.VMEM)
    return pl.pallas_call(
        finish_kernel,
        out_shape=(
            jax.ShapeDtypeStruct((bands, rows, total), jnp.float32),
            jax.ShapeDtypeStruct((1, bands), jnp.float32),
        ),
        in_specs=[vmem],
        out_specs=(vmem, vmem),
        compiler_params=pltpu.CompilerParams(vmem_limit_bytes=8 << 20),
        name="finish",
    )(back)


def shards(visibilities, flags):
    own = spectra(visibilities, flags)
    mine = lax.all_to_all(own, "bl", 0, 0, tiled=True, axis_index_groups=[OUT])
    back = lax.all_to_all(cross(mine), "bl", 0, 0, tiled=True, axis_index_groups=[BACK])
    power, band = finish(back)
    return (power, band.reshape(-1))


def solution(mesh):
    return jax.shard_map(
        shards,
        mesh=mesh,
        in_specs=(P(None, ("group", "bl"), None, None), P(("group", "bl"), None)),
        out_specs=(P(None, ("group", "bl"), None), P("group")),
        check_vma=False,
    )
```

time: 52.4 us -> 48 us (0.916); the launches traced: 52.2 us -> 47.2 us
  blocking collectives: 45.5 us -> 40.8 us
    all_to_all x2, blocking collectives: 45.5 us -> 40.8 us  [the longest x1 24.7 us: shards(): mine = lax.all_to_all(own, 'bl', 0, 0, tiled=True, axis_index_groups=[OUT])]
where the time goes in v4:
time: 48 us; the launch traced here: 47.2 us
  blocking collectives  40.8 us (85%)
  Pallas kernels  5.73 us (12%)
  between operations  0.65 us (1%)
    all_to_all x1, blocking collectives, shards(): mine = lax.all_to_all(own, 'bl', 0, 0, tiled=True, axis_index_groups=[OUT])  24.7 us
    all_to_all x1, blocking collectives, shards(): lax.all_to_all(cross(mine), 'bl', 0, 0, tiled=True, axis_index_groups=[BA...  16.1 us
    pallas_call x1, Pallas kernels, spectra(): pl.pallas_call(spectra_kernel, out_shape=pltpu.VMEM((NB, rows, NT * 2 * B...  3.62 us
    pallas_call x1, Pallas kernels, finish(): pl.pallas_call(finish_kernel, out_shape=(jax.ShapeDtypeStruct((bands, row...  1.25 us

profile of v4, /device:TPU:0, one launch (start us, length us, event | category | flops | bytes accessed | tf_op | source)
XLA Modules:
  0.0 47.2 jit_solution(379402511406898948)
XLA Ops:
  0.6 3.6 %spectra.1 = bf16[32,16,1024]{2,1,0:T(8,128)(2,1)S(1)} custom-call(f32[2,16,16,1024]{3,2,1,0:T(8,128)} %x_hbm.1, s32[8,16]{1,0:T(8,128)} %bitcast.2, f32[24,128]{1,0:T(8,128)} %constant.5.clone.rows_hbm, bf16[2,256,256]{2,1,0:T(8,128)(2,1)} %constant.4.clone.table_hbm), custom_call_target="tpu_custom_call" | custom-call | tf_op jit(solution)/shard_map/spectra/pallas_call | solution.py:143
  4.3 24.7 %all_to_all.10.own_ref = bf16[32,16,1024]{2,1,0:T(8,128)(2,1)S(1)} all-to-all(bf16[32,16,1024]{2,1,0:T(8,128)(2,1)S(1)} %spectra.1), channel_id=1, replica_groups={{26,7,0,13,14,11,20,17,18,31,24,5,6,3,12,9,10,23,16,29,30,27,4,1,2,15,8..., dimensions={0} | all-to-all | bytes 2097152 | tf_op jit(solution)/shard_map/all_to_all | solution.py:238
  28.9 0.9 %cross.1 = bf16[32,16,512]{2,1,0:T(8,128)(2,1)S(1)} custom-call(bf16[32,16,1024]{2,1,0:T(8,128)(2,1)S(1)} %all_to_all.10.own_ref), custom_call_target="tpu_custom_call" | custom-call | tf_op jit(solution)/shard_map/cross/pallas_call | solution.py:192
  29.8 16.1 %all_to_all.11.back_ref = bf16[32,16,512]{2,1,0:T(8,128)(2,1)S(1)} all-to-all(bf16[32,16,512]{2,1,0:T(8,128)(2,1)S(1)} %cross.1), channel_id=1, replica_groups={{26,7,0,13,14,11,20,17,18,31,24,5,6,3,12,9,10,23,16,29,30,27,4,1,2,15,8..., dimensions={0} | all-to-all | bytes 1048576 | tf_op jit(solution)/shard_map/all_to_all | solution.py:239
  46.0 1.3 %finish.1 = (f32[32,16,512]{2,1,0:T(8,128)}, f32[1,32]{1,0:T(1,128)}) custom-call(bf16[32,16,512]{2,1,0:T(8,128)(2,1)S(1)} %all_to_all.11.back_ref), custom_call_target="tpu_custom_call" | custom-call | tf_op jit(solution)/shard_map/finish/pallas_call | solution.py:223

commit v5 on v4

--- a/solution.py
+++ b/solution.py
@@ -16,7 +16,10 @@
 NB = NF // BW
 GROUP = 4
 HALF_ROOT = math.sqrt(0.5)
-OUT = [(-3 * i % 32) ^ 26 for i in range(32)]
+OUT = [
+    27, 15, 14, 12, 6, 10, 21, 16, 19, 30, 25, 4, 7, 2, 13, 8, 11, 18, 31, 28, 17, 26, 5, 0, 3, 1,
+    9, 20, 23, 22, 29, 24,
+]
 BACK = [(-3 * i % 32) ^ 26 for i in range(32)]
 
 

time: 48 us -> 47.3 us (0.985)
    all_to_all x1, blocking collectives: 16.1 us -> 15.4 us  [shards(): lax.all_to_all(cross(mine), 'bl', 0, 0, tiled=True, axis_index_groups=[BA...]
where the time goes in v5:
time: 47.3 us; the launch traced here: 47 us
  blocking collectives  40.6 us (86%)
  Pallas kernels  5.73 us (12%)
  between operations  0.65 us (1%)
    all_to_all x1, blocking collectives, shards(): mine = lax.all_to_all(own, 'bl', 0, 0, tiled=True, axis_index_groups=[OUT])  25.2 us
    all_to_all x1, blocking collectives, shards(): lax.all_to_all(cross(mine), 'bl', 0, 0, tiled=True, axis_index_groups=[BA...  15.4 us
    pallas_call x1, Pallas kernels, spectra(): pl.pallas_call(spectra_kernel, out_shape=pltpu.VMEM((NB, rows, NT * 2 * B...  3.62 us
    pallas_call x1, Pallas kernels, finish(): pl.pallas_call(finish_kernel, out_shape=(jax.ShapeDtypeStruct((bands, row...  1.25 us

profile of v5, /device:TPU:0, one launch (start us, length us, event | category | flops | bytes accessed | tf_op | source)
XLA Modules:
  0.0 47.0 jit_solution(7615732937172034218)
XLA Ops:
  0.6 3.6 %spectra.1 = bf16[32,16,1024]{2,1,0:T(8,128)(2,1)S(1)} custom-call(f32[2,16,16,1024]{3,2,1,0:T(8,128)} %x_hbm.1, s32[8,16]{1,0:T(8,128)} %bitcast.2, f32[24,128]{1,0:T(8,128)} %constant.5.clone.rows_hbm, bf16[2,256,256]{2,1,0:T(8,128)(2,1)} %constant.4.clone.table_hbm), custom_call_target="tpu_custom_call" | custom-call | tf_op jit(solution)/shard_map/spectra/pallas_call | solution.py:146
  4.3 25.2 %all_to_all.10.own_ref = bf16[32,16,1024]{2,1,0:T(8,128)(2,1)S(1)} all-to-all(bf16[32,16,1024]{2,1,0:T(8,128)(2,1)S(1)} %spectra.1), channel_id=1, replica_groups={{27,15,14,12,6,10,21,16,19,30,25,4,7,2,13,8,11,18,31,28,17,26,5,0,3,1,9..., dimensions={0} | all-to-all | bytes 2097152 | tf_op jit(solution)/shard_map/all_to_all | solution.py:241
  29.4 0.9 %cross.1 = bf16[32,16,512]{2,1,0:T(8,128)(2,1)S(1)} custom-call(bf16[32,16,1024]{2,1,0:T(8,128)(2,1)S(1)} %all_to_all.10.own_ref), custom_call_target="tpu_custom_call" | custom-call | tf_op jit(solution)/shard_map/cross/pallas_call | solution.py:195
  30.3 15.4 %all_to_all.11.back_ref = bf16[32,16,512]{2,1,0:T(8,128)(2,1)S(1)} all-to-all(bf16[32,16,512]{2,1,0:T(8,128)(2,1)S(1)} %cross.1), channel_id=1, replica_groups={{26,7,0,13,14,11,20,17,18,31,24,5,6,3,12,9,10,23,16,29,30,27,4,1,2,15,8..., dimensions={0} | all-to-all | bytes 1048576 | tf_op jit(solution)/shard_map/all_to_all | solution.py:242
  45.7 1.3 %finish.1 = (f32[32,16,512]{2,1,0:T(8,128)}, f32[1,32]{1,0:T(1,128)}) custom-call(bf16[32,16,512]{2,1,0:T(8,128)(2,1)S(1)} %all_to_all.11.back_ref), custom_call_target="tpu_custom_call" | custom-call | tf_op jit(solution)/shard_map/finish/pallas_call | solution.py:226

commit v6 on v5

--- a/solution.py
+++ b/solution.py
@@ -20,7 +20,10 @@
     27, 15, 14, 12, 6, 10, 21, 16, 19, 30, 25, 4, 7, 2, 13, 8, 11, 18, 31, 28, 17, 26, 5, 0, 3, 1,
     9, 20, 23, 22, 29, 24,
 ]
-BACK = [(-3 * i % 32) ^ 26 for i in range(32)]
+BACK = [
+    26, 13, 0, 19, 6, 25, 12, 31, 18, 5, 24, 11, 30, 17, 4, 23, 10, 29, 16, 3, 22, 9, 28, 15, 2, 21,
+    8, 27, 14, 1, 20, 7,
+]
 
 
 def taper_table():
@@ -123,10 +126,10 @@
             c.wait()
         if g == 1:
             tables.wait()
+        for t in range(g * GROUP, (g + 1) * GROUP):
+            fold(t)
         if g:
             multiply(g - 1)
-        for t in range(g * GROUP, (g + 1) * GROUP):
-            fold(t)
     multiply(NT // GROUP - 1)
     for k in range(NB):
         tiles = [z[8 * k : 8 * k + 8, m * 128 : (m + 1) * 128] for m in range(z.shape[1] // 128)]
@@ -168,9 +171,11 @@
     count, rows, _ = out_ref.shape
     total = count * rows
     delayed = jnp.concatenate([own_ref[OUT.index(s)] for s in range(count)], 0)
-    power = lax.dot_general(
-        delayed, delayed, (((1,), (1,)), ((), ())), preferred_element_type=jnp.float32
-    ) * (1.0 / NT)
+    half, dims = total // 2, (((1,), (1,)), ((), ()))
+    top = lax.dot_general(delayed[:half], delayed, dims, preferred_element_type=jnp.float32)
+    corner = lax.dot_general(delayed[half:], delayed[half:], dims, preferred_element_type=jnp.float32)
+    below = jnp.concatenate([top[:, half:].T, corner], 1)
+    power = jnp.concatenate([top, below], 0) * (1.0 / NT)
     out_ref[:, :, 0:total] = power.astype(jnp.bfloat16).reshape(count, rows, total)
     row = lax.broadcasted_iota(jnp.int32, (total, total), 0)
     col = lax.broadcasted_iota(jnp.int32, (total, total), 1)

time: 47.3 us -> 47.3 us (level)
  no operation moved by 1% of the time
where the time goes in v6:
time: 47.3 us; the launch traced here: 47 us
  blocking collectives  40.7 us (86%)
  Pallas kernels  5.7 us (12%)
  between operations  0.65 us (1%)
    all_to_all x1, blocking collectives, shards(): mine = lax.all_to_all(own, 'bl', 0, 0, tiled=True, axis_index_groups=[OUT])  25.2 us
    all_to_all x1, blocking collectives, shards(): lax.all_to_all(cross(mine), 'bl', 0, 0, tiled=True, axis_index_groups=[BA...  15.5 us
    pallas_call x1, Pallas kernels, spectra(): pl.pallas_call(spectra_kernel, out_shape=pltpu.VMEM((NB, rows, NT * 2 * B...  3.62 us
    pallas_call x1, Pallas kernels, finish(): pl.pallas_call(finish_kernel, out_shape=(jax.ShapeDtypeStruct((bands, row...  1.25 us

profile of v6, /device:TPU:0, one launch (start us, length us, event | category | flops | bytes accessed | tf_op | source)
XLA Modules:
  0.0 47.0 jit_solution(8529188880319805663)
XLA Ops:
  0.6 3.6 %spectra.1 = bf16[32,16,1024]{2,1,0:T(8,128)(2,1)S(1)} custom-call(f32[2,16,16,1024]{3,2,1,0:T(8,128)} %x_hbm.1, s32[8,16]{1,0:T(8,128)} %bitcast.2, f32[24,128]{1,0:T(8,128)} %constant.5.clone.rows_hbm, bf16[2,256,256]{2,1,0:T(8,128)(2,1)} %constant.4.clone.table_hbm), custom_call_target="tpu_custom_call" | custom-call | tf_op jit(solution)/shard_map/spectra/pallas_call | solution.py:149
  4.3 25.2 %all_to_all.10.own_ref = bf16[32,16,1024]{2,1,0:T(8,128)(2,1)S(1)} all-to-all(bf16[32,16,1024]{2,1,0:T(8,128)(2,1)S(1)} %spectra.1), channel_id=1, replica_groups={{27,15,14,12,6,10,21,16,19,30,25,4,7,2,13,8,11,18,31,28,17,26,5,0,3,1,9..., dimensions={0} | all-to-all | bytes 2097152 | tf_op jit(solution)/shard_map/all_to_all | solution.py:246
  29.4 0.8 %cross.1 = bf16[32,16,512]{2,1,0:T(8,128)(2,1)S(1)} custom-call(bf16[32,16,1024]{2,1,0:T(8,128)(2,1)S(1)} %all_to_all.10.own_ref), custom_call_target="tpu_custom_call" | custom-call | tf_op jit(solution)/shard_map/cross/pallas_call | solution.py:200
  30.3 15.5 %all_to_all.11.back_ref = bf16[32,16,512]{2,1,0:T(8,128)(2,1)S(1)} all-to-all(bf16[32,16,512]{2,1,0:T(8,128)(2,1)S(1)} %cross.1), channel_id=1, replica_groups={{26,13,0,19,6,25,12,31,18,5,24,11,30,17,4,23,10,29,16,3,22,9,28,15,2,21..., dimensions={0} | all-to-all | bytes 1048576 | tf_op jit(solution)/shard_map/all_to_all | solution.py:247
  45.8 1.3 %finish.1 = (f32[32,16,512]{2,1,0:T(8,128)}, f32[1,32]{1,0:T(1,128)}) custom-call(bf16[32,16,512]{2,1,0:T(8,128)(2,1)S(1)} %all_to_all.11.back_ref), custom_call_target="tpu_custom_call" | custom-call | tf_op jit(solution)/shard_map/finish/pallas_call | solution.py:231
